TPU v7x, 32 devices: a whole 2x2x4 slice. The times are simulated.
32 devices in a mesh: tm: 4 (over z), sx: 4 (over y, x), sy: 2 (over core).
Axes of the slice: x: 2, y: 2, z: 4, core: 2. Of those that a mesh axis runs over, the one named last changes fastest.
Arguments:
- thickness_guess: float32 [4, 1024, 256], P('tm', 'sx', 'sy'), may hold values from 0.5 to 1.5
- thickness_start: float32 [1024, 256], P('sx', 'sy'), may hold values from 0.5 to 1.5
- bed: float32 [1024, 256], P('sx', 'sy'), may hold values from -1.8 to 1.8
- rate_factor: float32 [1024, 256], P('sx', 'sy'), may hold values from 0.05 to 0.5
- mass_balance: float32 [4, 1024, 256], P('tm', 'sx', 'sy'), may hold values from -1.2 to 1.2
- cell_flags: int32 [1024, 256], P('sx', 'sy'), may hold values from 0 to 2, as said below
Outputs:
- thickness: float32 [4, 1024, 256], P('tm', 'sx', 'sy')
Inputs may be any that keep to these rules, and one draw needn't show every extreme that they name: `cell_flags`: 0 marks ice-free cells outside the glacier, 1 ice on bedrock, 2 ice on soft sediment.
All inputs are finite; a program needn't handle non-finite values.
Results may differ from a plain program's by a relative error of at most 0.00015.
Values sent between devices are 32-bit elements; how exact they have to be, the bound alone decides.
No kernel may reach another device: no remote copies, remote signals or barrier semaphores. Data moves between devices by JAX's collectives and lax.ppermute only.
A program may use at most 64 MiB of HBM per device.

v0:
```python
import math
import jax
import jax.numpy as jnp
from jax import lax
from jax.sharding import PartitionSpec as P

NEWTON = 2
SWEEPS = 8
circulant_weight = 0.25
time_step = 1.0
precise = lax.Precision.HIGHEST


def from_behind(value, axis, steps):
    count = lax.axis_size(axis)
    initial, last = (max(0, -steps), min(count, count - steps))
    return lax.ppermute(value, axis, [(source, source + steps) for source in range(initial, last)])


def extended(block, sides, width):
    for axis, dim in sides:
        count = lax.axis_size(axis)
        forward = [(i, i + 1) for i in range(count - 1)]
        backward = [(target, source) for source, target in forward]
        low = lax.ppermute(
            lax.slice_in_dim(block, block.shape[dim] - width, None, axis=dim), axis, forward
        )
        high = lax.ppermute(lax.slice_in_dim(block, 0, width, axis=dim), axis, backward)
        block = jnp.concatenate([low, block, high], axis=dim)
    return block


def cell_diffusivity(thickness, rate_factor, cell_flags):
    inside = (cell_flags != 0).astype(jnp.float32)
    boost = 1.0 + (cell_flags == 2).astype(jnp.float32)
    return inside * boost * rate_factor * thickness * thickness * jnp.abs(thickness)


def face_weights(padded):
    centre = padded[1:-1, 1:-1]
    return (
        0.5 * (centre + padded[2:, 1:-1]),
        0.5 * (centre + padded[:-2, 1:-1]),
        0.5 * (centre + padded[1:-1, 2:]),
        0.5 * (centre + padded[1:-1, :-2]),
    )


def neighbour_sum(weights, padded):
    return (
        weights[0] * padded[2:, 1:-1]
        + weights[1] * padded[:-2, 1:-1]
        + weights[2] * padded[1:-1, 2:]
        + weights[3] * padded[1:-1, :-2]
    )


def dft_tables(level_count):
    row_index = lax.broadcasted_iota(jnp.int32, (level_count, level_count), 0)
    col_index = lax.broadcasted_iota(jnp.int32, (level_count, level_count), 1)
    phase = 2.0 * math.pi / level_count * (row_index * col_index % level_count).astype(jnp.float32)
    return (jnp.cos(phase), jnp.sin(phase))


def forward_block(pieces):
    cosine, sine_table = dft_tables(pieces.shape[0])
    real_part = jnp.einsum("kl,lrc->krc", cosine, pieces, precision=precise)
    imag_part = -jnp.einsum("kl,lrc->krc", sine_table, pieces, precision=precise)
    return lax.all_to_all(
        jnp.stack([real_part, imag_part]), "tm", split_axis=1, concat_axis=2, tiled=True
    )


def inverse_block(pieces):
    level_count = pieces.shape[1]
    cosine, sine_table = dft_tables(level_count)
    values = (
        jnp.einsum("lk,krc->lrc", cosine, pieces[0], precision=precise)
        - jnp.einsum("lk,krc->lrc", sine_table, pieces[1], precision=precise)
    ) / level_count
    return lax.all_to_all(values, "tm", split_axis=0, concat_axis=1, tiled=True)


def window(matrix, offset, row_count, col_count):
    return matrix[offset : offset + row_count, offset : offset + col_count]


def jacobi_sweeps(source_wide, weights, coeffs, depth, row_count, col_count, grow):
    margin = depth
    value_real = source_wide[0] * coeffs[0] + source_wide[1] * coeffs[1]
    value_imag = source_wide[0] * coeffs[2] + source_wide[1] * coeffs[3]
    for sweep_index in range(SWEEPS - 1):
        if margin == 0:
            grown = grow(jnp.stack([value_real, value_imag]))
            value_real, value_imag = (grown[0], grown[1])
            margin = depth
        inner_margin = margin - 1
        offset = depth - inner_margin
        height = row_count + 2 * inner_margin
        breadth = col_count + 2 * inner_margin
        local_weights = tuple((window(member, offset, height, breadth) for member in weights))
        local_coeffs = tuple((window(member, offset, height, breadth) for member in coeffs))
        numer_real = window(source_wide[0], offset, height, breadth) + neighbour_sum(
            local_weights, value_real
        )
        numer_imag = window(source_wide[1], offset, height, breadth) + neighbour_sum(
            local_weights, value_imag
        )
        value_real = numer_real * local_coeffs[0] + numer_imag * local_coeffs[1]
        value_imag = numer_real * local_coeffs[2] + numer_imag * local_coeffs[3]
        margin = inner_margin
    return (
        window(value_real, margin, row_count, col_count),
        window(value_imag, margin, row_count, col_count),
    )


def body(thickness_guess, thickness_start, bed, rate_factor, mass_balance, cell_flags):
    level_count = lax.axis_size("tm")
    level_index = lax.axis_index("tm")
    depth = 4
    inside = (cell_flags != 0).astype(jnp.float32)
    ratio_root = circulant_weight ** (1.0 / level_count)
    angle = 2.0 * math.pi / level_count * level_index.astype(jnp.float32)
    shift_real = (1.0 - ratio_root * jnp.cos(angle)) / time_step
    shift_imag = ratio_root * jnp.sin(angle) / time_step
    lift_scale = ratio_root ** level_index.astype(jnp.float32)
    thickness = thickness_guess[0]
    balance = mass_balance[0]
    row_count, col_count = thickness.shape
    for newton_step in range(NEWTON):
        prior_level = from_behind(thickness, "tm", 1)
        prior_level = jnp.where(level_index == 0, thickness_start, prior_level)
        diffuse = cell_diffusivity(thickness, rate_factor, cell_flags)
        surface = thickness + bed
        padded = extended(jnp.stack([surface, diffuse]), (("sx", 1), ("sy", 2)), 1)
        weights = face_weights(padded[1])
        face_total = weights[0] + weights[1] + weights[2] + weights[3]
        change = (
            (thickness - prior_level) / time_step
            + face_total * surface
            - neighbour_sum(weights, padded[0])
            - balance
        )
        residual = inside * change
        mean_diff = lax.psum(diffuse, "tm") / level_count
        mean_rim = extended(jnp.stack([mean_diff, inside]), (("sx", 1), ("sy", 2)), depth + 1)
        mean_weights = face_weights(mean_rim[0])
        mean_total = mean_weights[0] + mean_weights[1] + mean_weights[2] + mean_weights[3]
        inside_wide = mean_rim[1][1:-1, 1:-1]
        denom_real = shift_real + mean_total
        denom_norm = denom_real * denom_real + shift_imag * shift_imag
        inverse_real = inside_wide * denom_real / denom_norm
        inverse_imag = -inside_wide * shift_imag / denom_norm
        source = residual * lift_scale
        spectrum = forward_block(
            lax.all_to_all(source[None], "tm", split_axis=1, concat_axis=0, tiled=True)
        )
        spectrum_real, spectrum_imag = (spectrum[0, 0], spectrum[1, 0])
        source_wide = extended(
            jnp.stack([spectrum_real, spectrum_imag]), (("sx", 1), ("sy", 2)), depth
        )

        def tile_extend(stacked):
            return extended(stacked, (("sx", 1), ("sy", 2)), depth)

        coeffs = (inverse_real, -inverse_imag, inverse_imag, inverse_real)
        solution_real, solution_imag = jacobi_sweeps(
            source_wide, mean_weights, coeffs, depth, row_count, col_count, tile_extend
        )
        update = inverse_block(
            lax.all_to_all(
                jnp.stack([solution_real, solution_imag])[:, None],
                "tm",
                split_axis=2,
                concat_axis=1,
                tiled=True,
            )
        )[0]
        thickness = thickness - update / lift_scale
    return thickness[None]


def solution(mesh):
    in_specs = (
        P("tm", "sx", "sy"),
        P("sx", "sy"),
        P("sx", "sy"),
        P("sx", "sy"),
        P("tm", "sx", "sy"),
        P("sx", "sy"),
    )
    out_specs = P("tm", "sx", "sy")
    return jax.shard_map(body, mesh=mesh, in_specs=in_specs, out_specs=out_specs, check_vma=False)
```

profile of v0, /device:TPU:0, one launch (start us, length us, event | category | flops | bytes accessed | tf_op | source)
XLA Modules:
  0.0 279.5 jit_solution(13134410729636757243)
XLA Ops:
  7.7 5.0 %collective-permute-start.1 = (f32[2,1,128]{2,1,0:T(1,128)S(1)}, f32[2,1,128]{2,1,0:T(1,128)S(1)}, u32[]{:S(2)}, u32[]{:S(2)}) collective-permute-start(f32[2,1,128]{2,1,0:T(1,128)S(1)} %get-tuple-element.131), channel_id=1, source_target_pairs={{0,2},{2,4},{4,6},{1,3},{3,5},{5,7},{8,10},{10,12},{12,14},{9,11},... | collective-permute-start | bytes 3080 | tf_op jit(solution)/shard_map/ppermute | solution.py:25
  14.1 3.5 %collective-permute-start = (f32[256,128]{1,0:T(8,128)S(1)}, f32[256,128]{1,0:T(8,128)S(1)}, u32[]{:S(2)}, u32[]{:S(2)}) collective-permute-start(f32[256,128]{1,0:T(8,128)S(1)} %bitcast.170), channel_id=1, source_target_pairs={{0,8},{8,16},{16,24},{1,9},{9,17},{17,25},{2,10},{10,18},{18,26},{... | collective-permute-start | bytes 393224 | tf_op jit(solution)/shard_map/ppermute | solution.py:17
  21.1 2.1 collective-permute-done.4
  26.2 4.9 %all-to-all-start = ((f32[1,256,128]{2,0,1:T(1,128)}), f32[1,256,128]{2,0,1:T(1,128)S(1)}, u32[]{:S(2)}, u32[]{:S(2)}) async-start(f32[1,256,128]{2,0,1:T(1,128)} %bitcast.8), calls=%async_computation | async-start | bytes 262144 | tf_op jit(solution)/shard_map/all_to_all | solution.py:157
  31.0 31.6 %all-reduce.3.cloned.1.call-done = f32[256,128]{1,0:T(8,128)} async-done(((f32[256,128]{1,0:T(8,128)}), f32[256,128]{1,0:T(8,128)}) %all-reduce.3.cloned.1.call-update) | async-done | bytes 131088 | tf_op jit(solution)/shard_map/psum | solution.py:146
  64.9 4.5 %collective-permute-start.9 = (f32[2,5,128]{2,1,0:T(8,128)S(1)}, f32[2,5,128]{2,1,0:T(8,128)S(1)}, u32[]{:S(2)}, u32[]{:S(2)}) collective-permute-start(f32[2,5,128]{2,1,0:T(8,128)S(1)} %get-tuple-element.136), channel_id=1, source_target_pairs={{0,2},{2,4},{4,6},{1,3},{3,5},{5,7},{8,10},{10,12},{12,14},{9,11},... | collective-permute-start | bytes 15368 | tf_op jit(solution)/shard_map/ppermute | solution.py:25
  71.1 3.4 %all-to-all-start.1 = ((f32[2,4,64,128]{3,2,0,1:T(8,128)}), f32[2,4,64,128]{3,2,0,1:T(8,128)S(1)}, u32[]{:S(2)}, u32[]{:S(2)}) async-start(f32[2,4,64,128]{3,2,0,1:T(8,128)} %copy.25), calls=%async_computation.1 | async-start | bytes 524288 | tf_op jit(solution)/shard_map/all_to_all | solution.py:69
  77.4 2.0 collective-permute-done.12
  81.3 4.3 %collective-permute-start.5 = (f32[2,4,128]{2,1,0:T(4,128)S(1)}, f32[2,4,128]{2,1,0:T(4,128)S(1)}, u32[]{:S(2)}, u32[]{:S(2)}) collective-permute-start(f32[2,4,128]{2,1,0:T(4,128)S(1)} %get-tuple-element.127), channel_id=1, source_target_pairs={{0,2},{2,4},{4,6},{1,3},{3,5},{5,7},{8,10},{10,12},{12,14},{9,11},... | collective-permute-start | bytes 12296 | tf_op jit(solution)/shard_map/ppermute | solution.py:25
  86.9 4.1 %collective-permute-done.6 = f32[2,4,128]{2,1,0:T(4,128)S(1)} collective-permute-done((f32[2,4,128]{2,1,0:T(4,128)S(1)}, f32[2,4,128]{2,1,0:T(4,128)S(1)}, u32[]{:S(2)}, u32[]{:S(2)}) %collective-permute-start.6) | collective-permute-done | bytes 4128 | tf_op jit(solution)/shard_map/ppermute | solution.py:28
  94.3 1.7 collective-permute-done.8
  101.1 3.4 %collective-permute-start.13 = (f32[2,4,128]{2,1,0:T(4,128)S(1)}, f32[2,4,128]{2,1,0:T(4,128)S(1)}, u32[]{:S(2)}, u32[]{:S(2)}) collective-permute-start(f32[2,4,128]{2,1,0:T(4,128)S(1)} %get-tuple-element.125), channel_id=1, source_target_pairs={{0,2},{2,4},{4,6},{1,3},{3,5},{5,7},{8,10},{10,12},{12,14},{9,11},... | collective-permute-start | bytes 12296 | tf_op jit(solution)/shard_map/ppermute | solution.py:25
  105.8 4.2 %collective-permute-done.14 = f32[2,4,128]{2,1,0:T(4,128)S(1)} collective-permute-done((f32[2,4,128]{2,1,0:T(4,128)S(1)}, f32[2,4,128]{2,1,0:T(4,128)S(1)}, u32[]{:S(2)}, u32[]{:S(2)}) %collective-permute-start.14) | collective-permute-done | bytes 4128 | tf_op jit(solution)/shard_map/ppermute | solution.py:28
  113.0 1.9 collective-permute-done.16
  119.3 12.5 %all_to_all.38 = f32[2,1,256,128]{3,0,1,2:T(2,128)S(1)} all-to-all(f32[2,1,256,128]{3,0,1,2:T(2,128)S(1)} %copy.28), channel_id=1, replica_groups=mesh['tm'=4,'sx'=4,'sy'=2] {'tm'}, dimensions={2} | all-to-all | bytes 524288 | tf_op jit(solution)/shard_map/all_to_all | solution.py:172
  132.9 8.5 %all_to_all.39 = f32[4,64,128]{2,1,0:T(8,128)S(1)} all-to-all(f32[4,64,128]{2,1,0:T(8,128)S(1)} %copy.33), channel_id=1, replica_groups=mesh['tm'=4,'sx'=4,'sy'=2] {'tm'}, dimensions={0} | all-to-all | bytes 262144 | tf_op jit(solution)/shard_map/all_to_all | solution.py:81
  142.4 2.8 %collective-permute-start.18 = (f32[2,1,128]{2,1,0:T(1,128)S(1)}, f32[2,1,128]{2,1,0:T(1,128)S(1)}, u32[]{:S(2)}, u32[]{:S(2)}) collective-permute-start(f32[2,1,128]{2,1,0:T(1,128)S(1)} %get-tuple-element.121), channel_id=1, source_target_pairs={{0,2},{2,4},{4,6},{1,3},{3,5},{5,7},{8,10},{10,12},{12,14},{9,11},... | collective-permute-start | bytes 3080 | tf_op jit(solution)/shard_map/ppermute | solution.py:25
  146.6 4.2 %collective-permute-done.19 = f32[2,1,128]{2,1,0:T(1,128)S(1)} collective-permute-done((f32[2,1,128]{2,1,0:T(1,128)S(1)}, f32[2,1,128]{2,1,0:T(1,128)S(1)}, u32[]{:S(2)}, u32[]{:S(2)}) %collective-permute-start.19) | collective-permute-done | bytes 1056 | tf_op jit(solution)/shard_map/ppermute | solution.py:28
  153.5 3.2 %collective-permute-start.17 = (f32[256,128]{1,0:T(8,128)S(1)}, f32[256,128]{1,0:T(8,128)S(1)}, u32[]{:S(2)}, u32[]{:S(2)}) collective-permute-start(f32[256,128]{1,0:T(8,128)S(1)} %get-tuple-element.33), channel_id=1, source_target_pairs={{0,8},{8,16},{16,24},{1,9},{9,17},{17,25},{2,10},{10,18},{18,26},{... | collective-permute-start | bytes 393224 | tf_op jit(solution)/shard_map/ppermute | solution.py:17
  157.8 2.6 collective-permute-done.17
  161.3 3.9 %all-to-all-start.4 = ((f32[1,256,128]{2,0,1:T(1,128)}), f32[1,256,128]{2,0,1:T(1,128)S(1)}, u32[]{:S(2)}, u32[]{:S(2)}) async-start(f32[1,256,128]{2,0,1:T(1,128)} %bitcast.37), calls=%async_computation.4 | async-start | bytes 262144 | tf_op jit(solution)/shard_map/all_to_all | solution.py:157
  165.2 27.1 %all-reduce.5.cloned.1.call-done = f32[256,128]{1,0:T(8,128)} async-done(((f32[256,128]{1,0:T(8,128)}), f32[256,128]{1,0:T(8,128)}) %all-reduce.5.cloned.1.call-update) | async-done | bytes 131088 | tf_op jit(solution)/shard_map/psum | solution.py:146
  193.3 3.4 %collective-permute-start.26 = (f32[2,5,128]{2,1,0:T(8,128)S(1)}, f32[2,5,128]{2,1,0:T(8,128)S(1)}, u32[]{:S(2)}, u32[]{:S(2)}) collective-permute-start(f32[2,5,128]{2,1,0:T(8,128)S(1)} %get-tuple-element.133), channel_id=1, source_target_pairs={{0,2},{2,4},{4,6},{1,3},{3,5},{5,7},{8,10},{10,12},{12,14},{9,11},... | collective-permute-start | bytes 15368 | tf_op jit(solution)/shard_map/ppermute | solution.py:25
  199.6 3.4 %all-to-all-start.5 = ((f32[2,4,64,128]{3,2,0,1:T(8,128)}), f32[2,4,64,128]{3,2,0,1:T(8,128)S(1)}, u32[]{:S(2)}, u32[]{:S(2)}) async-start(f32[2,4,64,128]{3,2,0,1:T(8,128)} %copy.37), calls=%async_computation.5 | async-start | bytes 524288 | tf_op jit(solution)/shard_map/all_to_all | solution.py:69
  205.8 2.1 collective-permute-done.29
  209.8 4.5 %collective-permute-start.22 = (f32[2,4,128]{2,1,0:T(4,128)S(1)}, f32[2,4,128]{2,1,0:T(4,128)S(1)}, u32[]{:S(2)}, u32[]{:S(2)}) collective-permute-start(f32[2,4,128]{2,1,0:T(4,128)S(1)} %get-tuple-element.117), channel_id=1, source_target_pairs={{0,2},{2,4},{4,6},{1,3},{3,5},{5,7},{8,10},{10,12},{12,14},{9,11},... | collective-permute-start | bytes 12296 | tf_op jit(solution)/shard_map/ppermute | solution.py:25
  215.7 4.5 %collective-permute-done.23 = f32[2,4,128]{2,1,0:T(4,128)S(1)} collective-permute-done((f32[2,4,128]{2,1,0:T(4,128)S(1)}, f32[2,4,128]{2,1,0:T(4,128)S(1)}, u32[]{:S(2)}, u32[]{:S(2)}) %collective-permute-start.23) | collective-permute-done | bytes 4128 | tf_op jit(solution)/shard_map/ppermute | solution.py:28
  230.3 4.8 %collective-permute-start.30 = (f32[2,4,128]{2,1,0:T(4,128)S(1)}, f32[2,4,128]{2,1,0:T(4,128)S(1)}, u32[]{:S(2)}, u32[]{:S(2)}) collective-permute-start(f32[2,4,128]{2,1,0:T(4,128)S(1)} %get-tuple-element.115), channel_id=1, source_target_pairs={{0,2},{2,4},{4,6},{1,3},{3,5},{5,7},{8,10},{10,12},{12,14},{9,11},... | collective-permute-start | bytes 12296 | tf_op jit(solution)/shard_map/ppermute | solution.py:25
  236.4 4.2 %collective-permute-done.31 = f32[2,4,128]{2,1,0:T(4,128)S(1)} collective-permute-done((f32[2,4,128]{2,1,0:T(4,128)S(1)}, f32[2,4,128]{2,1,0:T(4,128)S(1)}, u32[]{:S(2)}, u32[]{:S(2)}) %collective-permute-start.31) | collective-permute-done | bytes 4128 | tf_op jit(solution)/shard_map/ppermute | solution.py:28
  243.4 2.1 collective-permute-done.33
  249.9 12.5 %all_to_all.80 = f32[2,1,256,128]{3,0,1,2:T(2,128)S(1)} all-to-all(f32[2,1,256,128]{3,0,1,2:T(2,128)S(1)} %copy.40), channel_id=1, replica_groups=mesh['tm'=4,'sx'=4,'sy'=2] {'tm'}, dimensions={2} | all-to-all | bytes 524288 | tf_op jit(solution)/shard_map/all_to_all | solution.py:172
  263.5 8.5 %all_to_all.81 = f32[4,64,128]{2,1,0:T(8,128)S(1)} all-to-all(f32[4,64,128]{2,1,0:T(8,128)S(1)} %copy.45), channel_id=1, replica_groups=mesh['tm'=4,'sx'=4,'sy'=2] {'tm'}, dimensions={0} | all-to-all | bytes 262144 | tf_op jit(solution)/shard_map/all_to_all | solution.py:81
  (177 shorter events, 73.5 us)
Async XLA Ops:
  7.7 9.8 %collective-permute-start.1 = (f32[2,1,128]{2,1,0:T(1,128)S(1)}, f32[2,1,128]{2,1,0:T(1,128)S(1)}, u32[]{:S(2)}, u32[]{:S(2)}) collective-permute-start(f32[2,1,128]{2,1,0:T(1,128)S(1)} %get-tuple-element.131), channel_id=1, source_target_pairs={{0,2},{2,4},{4,6},{1,3},{3,5},{5,7},{8,10},{10,12},{12,14},{9,11},... | collective-permute-start | bytes 3080 | tf_op jit(solution)/shard_map/ppermute | solution.py:25
  12.7 5.5 %collective-permute-start.2 = (f32[2,1,128]{2,1,0:T(1,128)S(1)}, f32[2,1,128]{2,1,0:T(1,128)S(1)}, u32[]{:S(2)}, u32[]{:S(2)}) collective-permute-start(f32[2,1,128]{2,1,0:T(1,128)S(1)} %get-tuple-element.132), channel_id=1, source_target_pairs={{2,0},{4,2},{6,4},{3,1},{5,3},{7,5},{10,8},{12,10},{14,12},{11,9},... | collective-permute-start | bytes 3080 | tf_op jit(solution)/shard_map/ppermute | solution.py:28
  14.1 10.2 %collective-permute-start = (f32[256,128]{1,0:T(8,128)S(1)}, f32[256,128]{1,0:T(8,128)S(1)}, u32[]{:S(2)}, u32[]{:S(2)}) collective-permute-start(f32[256,128]{1,0:T(8,128)S(1)} %bitcast.170), channel_id=1, source_target_pairs={{0,8},{8,16},{16,24},{1,9},{9,17},{17,25},{2,10},{10,18},{18,26},{... | collective-permute-start | bytes 393224 | tf_op jit(solution)/shard_map/ppermute | solution.py:17
  19.7 3.4 %collective-permute-start.4 = (f32[2,258,1]{2,1,0:T(8,128)S(1)}, f32[2,258,1]{2,1,0:T(8,128)S(1)}, u32[]{:S(2)}, u32[]{:S(2)}) collective-permute-start(f32[2,258,1]{2,1,0:T(8,128)S(1)} %get-tuple-element.112), channel_id=1, source_target_pairs={{1,0},{3,2},{5,4},{7,6},{9,8},{11,10},{13,12},{15,14},{17,16},{19,... | collective-permute-start | bytes 6200 | tf_op jit(solution)/shard_map/ppermute | solution.py:28
  23.4 39.2 %all-reduce.3.cloned.1.call-start = ((), (), s32[]{:S(2)}) async-start(), calls=%async_computation.8 | async-start | bytes 262144 | tf_op jit(solution)/shard_map/psum | solution.py:146
  26.2 43.2 %all-to-all-start = ((f32[1,256,128]{2,0,1:T(1,128)}), f32[1,256,128]{2,0,1:T(1,128)S(1)}, u32[]{:S(2)}, u32[]{:S(2)}) async-start(f32[1,256,128]{2,0,1:T(1,128)} %bitcast.8), calls=%async_computation | async-start | bytes 262144 | tf_op jit(solution)/shard_map/all_to_all | solution.py:157
  63.6 10.9 %collective-permute-start.10 = (f32[2,5,128]{2,1,0:T(8,128)S(1)}, f32[2,5,128]{2,1,0:T(8,128)S(1)}, u32[]{:S(2)}, u32[]{:S(2)}) collective-permute-start(f32[2,5,128]{2,1,0:T(8,128)S(1)} %get-tuple-element.61), channel_id=1, source_target_pairs={{2,0},{4,2},{6,4},{3,1},{5,3},{7,5},{10,8},{12,10},{14,12},{11,9},... | collective-permute-start | bytes 15368 | tf_op jit(solution)/shard_map/ppermute | solution.py:28
  64.9 9.6 %collective-permute-start.9 = (f32[2,5,128]{2,1,0:T(8,128)S(1)}, f32[2,5,128]{2,1,0:T(8,128)S(1)}, u32[]{:S(2)}, u32[]{:S(2)}) collective-permute-start(f32[2,5,128]{2,1,0:T(8,128)S(1)} %get-tuple-element.136), channel_id=1, source_target_pairs={{0,2},{2,4},{4,6},{1,3},{3,5},{5,7},{8,10},{10,12},{12,14},{9,11},... | collective-permute-start | bytes 15368 | tf_op jit(solution)/shard_map/ppermute | solution.py:25
  71.1 10.2 %all-to-all-start.1 = ((f32[2,4,64,128]{3,2,0,1:T(8,128)}), f32[2,4,64,128]{3,2,0,1:T(8,128)S(1)}, u32[]{:S(2)}, u32[]{:S(2)}) async-start(f32[2,4,64,128]{3,2,0,1:T(8,128)} %copy.25), calls=%async_computation.1 | async-start | bytes 524288 | tf_op jit(solution)/shard_map/all_to_all | solution.py:69
  76.0 3.5 %collective-permute-start.12 = (f32[2,266,5]{2,1,0:T(8,128)S(1)}, f32[2,266,5]{2,1,0:T(8,128)S(1)}, u32[]{:S(2)}, u32[]{:S(2)}) collective-permute-start(f32[2,266,5]{2,1,0:T(8,128)S(1)} %get-tuple-element.92), channel_id=1, source_target_pairs={{1,0},{3,2},{5,4},{7,6},{9,8},{11,10},{13,12},{15,14},{17,16},{19,... | collective-permute-start | bytes 31928 | tf_op jit(solution)/shard_map/ppermute | solution.py:28
  81.3 5.6 %collective-permute-start.5 = (f32[2,4,128]{2,1,0:T(4,128)S(1)}, f32[2,4,128]{2,1,0:T(4,128)S(1)}, u32[]{:S(2)}, u32[]{:S(2)}) collective-permute-start(f32[2,4,128]{2,1,0:T(4,128)S(1)} %get-tuple-element.127), channel_id=1, source_target_pairs={{0,2},{2,4},{4,6},{1,3},{3,5},{5,7},{8,10},{10,12},{12,14},{9,11},... | collective-permute-start | bytes 12296 | tf_op jit(solution)/shard_map/ppermute | solution.py:25
  85.5 5.5 %collective-permute-start.6 = (f32[2,4,128]{2,1,0:T(4,128)S(1)}, f32[2,4,128]{2,1,0:T(4,128)S(1)}, u32[]{:S(2)}, u32[]{:S(2)}) collective-permute-start(f32[2,4,128]{2,1,0:T(4,128)S(1)} %get-tuple-element.128), channel_id=1, source_target_pairs={{2,0},{4,2},{6,4},{3,1},{5,3},{7,5},{10,8},{12,10},{14,12},{11,9},... | collective-permute-start | bytes 12296 | tf_op jit(solution)/shard_map/ppermute | solution.py:28
  92.5 3.4 %collective-permute-start.8 = (f32[2,264,4]{2,1,0:T(8,128)S(1)}, f32[2,264,4]{2,1,0:T(8,128)S(1)}, u32[]{:S(2)}, u32[]{:S(2)}) collective-permute-start(f32[2,264,4]{2,1,0:T(8,128)S(1)} %get-tuple-element.110), channel_id=1, source_target_pairs={{1,0},{3,2},{5,4},{7,6},{9,8},{11,10},{13,12},{15,14},{17,16},{19,... | collective-permute-start | bytes 25352 | tf_op jit(solution)/shard_map/ppermute | solution.py:28
  101.1 4.7 %collective-permute-start.13 = (f32[2,4,128]{2,1,0:T(4,128)S(1)}, f32[2,4,128]{2,1,0:T(4,128)S(1)}, u32[]{:S(2)}, u32[]{:S(2)}) collective-permute-start(f32[2,4,128]{2,1,0:T(4,128)S(1)} %get-tuple-element.125), channel_id=1, source_target_pairs={{0,2},{2,4},{4,6},{1,3},{3,5},{5,7},{8,10},{10,12},{12,14},{9,11},... | collective-permute-start | bytes 12296 | tf_op jit(solution)/shard_map/ppermute | solution.py:25
  104.5 5.5 %collective-permute-start.14 = (f32[2,4,128]{2,1,0:T(4,128)S(1)}, f32[2,4,128]{2,1,0:T(4,128)S(1)}, u32[]{:S(2)}, u32[]{:S(2)}) collective-permute-start(f32[2,4,128]{2,1,0:T(4,128)S(1)} %get-tuple-element.126), channel_id=1, source_target_pairs={{2,0},{4,2},{6,4},{3,1},{5,3},{7,5},{10,8},{12,10},{14,12},{11,9},... | collective-permute-start | bytes 12296 | tf_op jit(solution)/shard_map/ppermute | solution.py:28
  111.5 3.4 %collective-permute-start.16 = (f32[2,264,4]{2,1,0:T(8,128)S(1)}, f32[2,264,4]{2,1,0:T(8,128)S(1)}, u32[]{:S(2)}, u32[]{:S(2)}) collective-permute-start(f32[2,264,4]{2,1,0:T(8,128)S(1)} %get-tuple-element.107), channel_id=1, source_target_pairs={{1,0},{3,2},{5,4},{7,6},{9,8},{11,10},{13,12},{15,14},{17,16},{19,... | collective-permute-start | bytes 25352 | tf_op jit(solution)/shard_map/ppermute | solution.py:28
  142.4 4.1 %collective-permute-start.18 = (f32[2,1,128]{2,1,0:T(1,128)S(1)}, f32[2,1,128]{2,1,0:T(1,128)S(1)}, u32[]{:S(2)}, u32[]{:S(2)}) collective-permute-start(f32[2,1,128]{2,1,0:T(1,128)S(1)} %get-tuple-element.121), channel_id=1, source_target_pairs={{0,2},{2,4},{4,6},{1,3},{3,5},{5,7},{8,10},{10,12},{12,14},{9,11},... | collective-permute-start | bytes 3080 | tf_op jit(solution)/shard_map/ppermute | solution.py:25
  145.3 5.5 %collective-permute-start.19 = (f32[2,1,128]{2,1,0:T(1,128)S(1)}, f32[2,1,128]{2,1,0:T(1,128)S(1)}, u32[]{:S(2)}, u32[]{:S(2)}) collective-permute-start(f32[2,1,128]{2,1,0:T(1,128)S(1)} %get-tuple-element.122), channel_id=1, source_target_pairs={{2,0},{4,2},{6,4},{3,1},{5,3},{7,5},{10,8},{12,10},{14,12},{11,9},... | collective-permute-start | bytes 3080 | tf_op jit(solution)/shard_map/ppermute | solution.py:28
  150.9 5.8 %collective-permute-start.20 = (f32[2,258,1]{2,1,0:T(8,128)S(1)}, f32[2,258,1]{2,1,0:T(8,128)S(1)}, u32[]{:S(2)}, u32[]{:S(2)}) collective-permute-start(f32[2,258,1]{2,1,0:T(8,128)S(1)} %get-tuple-element.101), channel_id=1, source_target_pairs={{0,1},{2,3},{4,5},{6,7},{8,9},{10,11},{12,13},{14,15},{16,17},{18,... | collective-permute-start | bytes 6200 | tf_op jit(solution)/shard_map/ppermute | solution.py:25
  152.2 4.5 %collective-permute-start.21 = (f32[2,258,1]{2,1,0:T(8,128)S(1)}, f32[2,258,1]{2,1,0:T(8,128)S(1)}, u32[]{:S(2)}, u32[]{:S(2)}) collective-permute-start(f32[2,258,1]{2,1,0:T(8,128)S(1)} %get-tuple-element.102), channel_id=1, source_target_pairs={{1,0},{3,2},{5,4},{7,6},{9,8},{11,10},{13,12},{15,14},{17,16},{19,... | collective-permute-start | bytes 6200 | tf_op jit(solution)/shard_map/ppermute | solution.py:28
  153.5 6.9 %collective-permute-start.17 = (f32[256,128]{1,0:T(8,128)S(1)}, f32[256,128]{1,0:T(8,128)S(1)}, u32[]{:S(2)}, u32[]{:S(2)}) collective-permute-start(f32[256,128]{1,0:T(8,128)S(1)} %get-tuple-element.33), channel_id=1, source_target_pairs={{0,8},{8,16},{16,24},{1,9},{9,17},{17,25},{2,10},{10,18},{18,26},{... | collective-permute-start | bytes 393224 | tf_op jit(solution)/shard_map/ppermute | solution.py:17
  157.0 35.3 %all-reduce.5.cloned.1.call-start = ((), (), s32[]{:S(2)}) async-start(), calls=%async_computation.9 | async-start | bytes 262144 | tf_op jit(solution)/shard_map/psum | solution.py:146
  161.3 36.6 %all-to-all-start.4 = ((f32[1,256,128]{2,0,1:T(1,128)}), f32[1,256,128]{2,0,1:T(1,128)S(1)}, u32[]{:S(2)}, u32[]{:S(2)}) async-start(f32[1,256,128]{2,0,1:T(1,128)} %bitcast.37), calls=%async_computation.4 | async-start | bytes 262144 | tf_op jit(solution)/shard_map/all_to_all | solution.py:157
  193.3 9.7 %collective-permute-start.26 = (f32[2,5,128]{2,1,0:T(8,128)S(1)}, f32[2,5,128]{2,1,0:T(8,128)S(1)}, u32[]{:S(2)}, u32[]{:S(2)}) collective-permute-start(f32[2,5,128]{2,1,0:T(8,128)S(1)} %get-tuple-element.133), channel_id=1, source_target_pairs={{0,2},{2,4},{4,6},{1,3},{3,5},{5,7},{8,10},{10,12},{12,14},{9,11},... | collective-permute-start | bytes 15368 | tf_op jit(solution)/shard_map/ppermute | solution.py:25
  196.6 6.4 %collective-permute-start.27 = (f32[2,5,128]{2,1,0:T(8,128)S(1)}, f32[2,5,128]{2,1,0:T(8,128)S(1)}, u32[]{:S(2)}, u32[]{:S(2)}) collective-permute-start(f32[2,5,128]{2,1,0:T(8,128)S(1)} %get-tuple-element.134), channel_id=1, source_target_pairs={{2,0},{4,2},{6,4},{3,1},{5,3},{7,5},{10,8},{12,10},{14,12},{11,9},... | collective-permute-start | bytes 15368 | tf_op jit(solution)/shard_map/ppermute | solution.py:28
  199.6 10.2 %all-to-all-start.5 = ((f32[2,4,64,128]{3,2,0,1:T(8,128)}), f32[2,4,64,128]{3,2,0,1:T(8,128)S(1)}, u32[]{:S(2)}, u32[]{:S(2)}) async-start(f32[2,4,64,128]{3,2,0,1:T(8,128)} %copy.37), calls=%async_computation.5 | async-start | bytes 524288 | tf_op jit(solution)/shard_map/all_to_all | solution.py:69
  204.5 3.5 %collective-permute-start.29 = (f32[2,266,5]{2,1,0:T(8,128)S(1)}, f32[2,266,5]{2,1,0:T(8,128)S(1)}, u32[]{:S(2)}, u32[]{:S(2)}) collective-permute-start(f32[2,266,5]{2,1,0:T(8,128)S(1)} %get-tuple-element.90), channel_id=1, source_target_pairs={{1,0},{3,2},{5,4},{7,6},{9,8},{11,10},{13,12},{15,14},{17,16},{19,... | collective-permute-start | bytes 31928 | tf_op jit(solution)/shard_map/ppermute | solution.py:28
  209.8 5.9 %collective-permute-start.22 = (f32[2,4,128]{2,1,0:T(4,128)S(1)}, f32[2,4,128]{2,1,0:T(4,128)S(1)}, u32[]{:S(2)}, u32[]{:S(2)}) collective-permute-start(f32[2,4,128]{2,1,0:T(4,128)S(1)} %get-tuple-element.117), channel_id=1, source_target_pairs={{0,2},{2,4},{4,6},{1,3},{3,5},{5,7},{8,10},{10,12},{12,14},{9,11},... | collective-permute-start | bytes 12296 | tf_op jit(solution)/shard_map/ppermute | solution.py:25
  214.3 5.9 %collective-permute-start.23 = (f32[2,4,128]{2,1,0:T(4,128)S(1)}, f32[2,4,128]{2,1,0:T(4,128)S(1)}, u32[]{:S(2)}, u32[]{:S(2)}) collective-permute-start(f32[2,4,128]{2,1,0:T(4,128)S(1)} %get-tuple-element.118), channel_id=1, source_target_pairs={{2,0},{4,2},{6,4},{3,1},{5,3},{7,5},{10,8},{12,10},{14,12},{11,9},... | collective-permute-start | bytes 12296 | tf_op jit(solution)/shard_map/ppermute | solution.py:28
  221.7 3.4 %collective-permute-start.25 = (f32[2,264,4]{2,1,0:T(8,128)S(1)}, f32[2,264,4]{2,1,0:T(8,128)S(1)}, u32[]{:S(2)}, u32[]{:S(2)}) collective-permute-start(f32[2,264,4]{2,1,0:T(8,128)S(1)} %get-tuple-element.100), channel_id=1, source_target_pairs={{1,0},{3,2},{5,4},{7,6},{9,8},{11,10},{13,12},{15,14},{17,16},{19,... | collective-permute-start | bytes 25352 | tf_op jit(solution)/shard_map/ppermute | solution.py:28
  230.3 6.1 %collective-permute-start.30 = (f32[2,4,128]{2,1,0:T(4,128)S(1)}, f32[2,4,128]{2,1,0:T(4,128)S(1)}, u32[]{:S(2)}, u32[]{:S(2)}) collective-permute-start(f32[2,4,128]{2,1,0:T(4,128)S(1)} %get-tuple-element.115), channel_id=1, source_target_pairs={{0,2},{2,4},{4,6},{1,3},{3,5},{5,7},{8,10},{10,12},{12,14},{9,11},... | collective-permute-start | bytes 12296 | tf_op jit(solution)/shard_map/ppermute | solution.py:25
  235.1 5.5 %collective-permute-start.31 = (f32[2,4,128]{2,1,0:T(4,128)S(1)}, f32[2,4,128]{2,1,0:T(4,128)S(1)}, u32[]{:S(2)}, u32[]{:S(2)}) collective-permute-start(f32[2,4,128]{2,1,0:T(4,128)S(1)} %get-tuple-element.116), channel_id=1, source_target_pairs={{2,0},{4,2},{6,4},{3,1},{5,3},{7,5},{10,8},{12,10},{14,12},{11,9},... | collective-permute-start | bytes 12296 | tf_op jit(solution)/shard_map/ppermute | solution.py:28
  (16 other events, 64.1 us)
Sparse Core Ops, SparseCore 0:
  26.6 36.0 all-reduce.2
  160.1 32.1 all-reduce.4
where the time goes:
time: 281 us; the launch traced here: 279 us
  waiting for transfers between devices  101 us (36%)
  starting transfers between devices  86.6 us (31%)
  blocking collectives  42 us (15%)
  other arithmetic  26.4 us (9%)
  between operations  14.7 us (5%)
  local copies, waits for them, and re-layouts  5.55 us (2%)
  matrix products  3.35 us (1%)
    psum x2, waiting for transfers between devices, body(): mean_diff = lax.psum(diffuse, 'tm') / level_count  58.7 us
    ppermute x16, starting transfers between devices, extended(): lax.ppermute(lax.slice_in_dim(block, block.shape[dim] - width, None, axis...  43.2 us
    ppermute x16, waiting for transfers between devices, extended(): lax.ppermute(lax.slice_in_dim(block, 0, width, axis=dim), axis, backward)  35.3 us
    all_to_all x2, blocking collectives, body(): lax.all_to_all(jnp.stack([solution_real, solution_imag])[:, None], 'tm',...  25.1 us
    ppermute x16, starting transfers between devices, extended(): lax.ppermute(lax.slice_in_dim(block, 0, width, axis=dim), axis, backward)  21.1 us
    all_to_all x2, blocking collectives, inverse_block(): return lax.all_to_all(values, 'tm', split_axis=0, concat_axis=1, tiled=True)  16.9 us
    all_to_all x2, starting transfers between devices, body(): lax.all_to_all(source[None], 'tm', split_axis=1, concat_axis=0, tiled=True)  8.76 us
    add x8, other arithmetic, jacobi_sweeps(): value_real = numer_real * local_coeffs[0] + numer_imag * local_coeffs[1]  8.62 us
  transfers between devices with their start and end apart: 40, of which 18 were waited for; matrix products, arithmetic and copies ran while one was open for 3% of the time, Pallas kernels for 0%

commit v1 on v0

--- a/solution.py
+++ b/solution.py
@@ -143,7 +143,7 @@
             - balance
         )
         residual = inside * change
-        mean_diff = lax.psum(diffuse, "tm") / level_count
+        mean_diff = jnp.sum(lax.all_gather(diffuse, "tm"), axis=0) / level_count
         mean_rim = extended(jnp.stack([mean_diff, inside]), (("sx", 1), ("sy", 2)), depth + 1)
         mean_weights = face_weights(mean_rim[0])
         mean_total = mean_weights[0] + mean_weights[1] + mean_weights[2] + mean_weights[3]

time: 281 us -> 237 us (0.84)
  waiting for transfers between devices: 101 us -> 39.5 us
  blocking collectives: 42 us -> 71.8 us
  between operations: 14.7 us -> 1.26 us
  starting transfers between devices: 86.6 us -> 89.5 us
    psum x2 -> x0, waiting for transfers between devices: 58.7 us -> none  [body(): mean_diff = lax.psum(diffuse, 'tm') / level_count]
    all_gather x0 -> x2, blocking collectives: none -> 31.3 us  [body(): mean_diff = jnp.sum(lax.all_gather(diffuse, 'tm'), axis=0) / level_count]
    all_to_all x2, waiting for transfers between devices: 3 us -> 6.73 us  [forward_block(): lax.all_to_all(jnp.stack([real_part, imag_part]), 'tm', split_axis=1, con...]
    ppermute x16, waiting for transfers between devices: 35.3 us -> 32.2 us  [extended(): lax.ppermute(lax.slice_in_dim(block, 0, width, axis=dim), axis, backward)]
  transfers between devices with their start and end apart: 40 -> 38, of which waited for: 18 -> 15; matrix products, arithmetic and copies ran while one was open for 3% -> 3% of each run, Pallas kernels for 0% -> 0%
where the time goes in v1:
time: 237 us; the launch traced here: 236 us
  starting transfers between devices  89.5 us (38%)
  blocking collectives  71.8 us (30%)
  waiting for transfers between devices  39.5 us (17%)
  other arithmetic  24.8 us (10%)
  local copies, waits for them, and re-layouts  5.62 us (2%)
  matrix products  3.34 us (1%)
    ppermute x16, starting transfers between devices, extended(): lax.ppermute(lax.slice_in_dim(block, block.shape[dim] - width, None, axis...  44.1 us
    ppermute x16, waiting for transfers between devices, extended(): lax.ppermute(lax.slice_in_dim(block, 0, width, axis=dim), axis, backward)  32.2 us
    all_gather x2, blocking collectives, body(): mean_diff = jnp.sum(lax.all_gather(diffuse, 'tm'), axis=0) / level_count  31.3 us
    all_to_all x2, blocking collectives, body(): lax.all_to_all(jnp.stack([solution_real, solution_imag])[:, None], 'tm',...  23.7 us
    ppermute x16, starting transfers between devices, extended(): lax.ppermute(lax.slice_in_dim(block, 0, width, axis=dim), axis, backward)  21.1 us
    all_to_all x2, blocking collectives, inverse_block(): return lax.all_to_all(values, 'tm', split_axis=0, concat_axis=1, tiled=True)  16.9 us
    all_to_all x2, starting transfers between devices, forward_block(): lax.all_to_all(jnp.stack([real_part, imag_part]), 'tm', split_axis=1, con...  9.59 us
    add x8, other arithmetic, jacobi_sweeps(): value_real = numer_real * local_coeffs[0] + numer_imag * local_coeffs[1]  8.63 us
  transfers between devices with their start and end apart: 38, of which 15 were waited for; matrix products, arithmetic and copies ran while one was open for 3% of the time, Pallas kernels for 0%

profile of v1, /device:TPU:0, one launch (start us, length us, event | category | flops | bytes accessed | tf_op | source)
XLA Modules:
  0.0 235.9 jit_solution(11954882806305019232)
XLA Ops:
  0.0 5.0 %collective-permute-start = (f32[256,128]{1,0:T(8,128)}, f32[256,128]{1,0:T(8,128)S(1)}, u32[]{:S(2)}, u32[]{:S(2)}) collective-permute-start(f32[256,128]{1,0:T(8,128)} %bitcast.172), channel_id=1, source_target_pairs={{0,8},{8,16},{16,24},{1,9},{9,17},{17,25},{2,10},{10,18},{18,26},{... | collective-permute-start | bytes 393224 | tf_op jit(solution)/shard_map/ppermute | solution.py:17
  6.1 3.4 %collective-permute-start.1 = (f32[2,1,128]{2,1,0:T(1,128)S(1)}, f32[2,1,128]{2,1,0:T(1,128)S(1)}, u32[]{:S(2)}, u32[]{:S(2)}) collective-permute-start(f32[2,1,128]{2,1,0:T(1,128)S(1)} %get-tuple-element.131), channel_id=1, source_target_pairs={{0,2},{2,4},{4,6},{1,3},{3,5},{5,7},{8,10},{10,12},{12,14},{9,11},... | collective-permute-start | bytes 3080 | tf_op jit(solution)/shard_map/ppermute | solution.py:25
  10.8 16.4 %all-gather = f32[1024,128]{1,0:T(8,128)S(1)} all-gather(f32[256,128]{1,0:T(8,128)S(1)} %get-tuple-element.63), channel_id=2, replica_groups=mesh['tm'=4,'sx'=4,'sy'=2] {'tm'}, dimensions={0}, use_global_device_ids=true | all-gather | bytes 655360 | tf_op jit(solution)/shard_map/all_gather | solution.py:146
  30.1 2.1 collective-permute-done.4
  34.6 3.3 %all-to-all-start = ((f32[1,256,128]{2,0,1:T(1,128)}), f32[1,256,128]{2,0,1:T(1,128)S(1)}, u32[]{:S(2)}, u32[]{:S(2)}) async-start(f32[1,256,128]{2,0,1:T(1,128)} %bitcast.8), calls=%async_computation | async-start | bytes 262144 | tf_op jit(solution)/shard_map/all_to_all | solution.py:157
  39.2 5.2 %collective-permute-start.9 = (f32[2,5,128]{2,1,0:T(8,128)S(1)}, f32[2,5,128]{2,1,0:T(8,128)S(1)}, u32[]{:S(2)}, u32[]{:S(2)}) collective-permute-start(f32[2,5,128]{2,1,0:T(8,128)S(1)} %get-tuple-element.136), channel_id=1, source_target_pairs={{0,2},{2,4},{4,6},{1,3},{3,5},{5,7},{8,10},{10,12},{12,14},{9,11},... | collective-permute-start | bytes 15368 | tf_op jit(solution)/shard_map/ppermute | solution.py:25
  46.1 5.1 %all-to-all-start.1 = ((f32[2,4,64,128]{3,2,0,1:T(8,128)}), f32[2,4,64,128]{3,2,0,1:T(8,128)S(1)}, u32[]{:S(2)}, u32[]{:S(2)}) async-start(f32[2,4,64,128]{3,2,0,1:T(8,128)} %copy.25), calls=%async_computation.1 | async-start | bytes 524288 | tf_op jit(solution)/shard_map/all_to_all | solution.py:69
  54.1 2.0 collective-permute-done.12
  56.4 3.4 %all-to-all-done.1 = f32[2,4,64,128]{3,2,0,1:T(8,128)S(1)} async-done(((f32[2,4,64,128]{3,2,0,1:T(8,128)}), f32[2,4,64,128]{3,2,0,1:T(8,128)S(1)}, u32[]{:S(2)}, u32[]{:S(2)}) %all-to-all-start.1) | async-done | bytes 262176 | tf_op jit(solution)/shard_map/all_to_all | solution.py:69
  59.8 4.5 %collective-permute-start.5 = (f32[2,4,128]{2,1,0:T(4,128)S(1)}, f32[2,4,128]{2,1,0:T(4,128)S(1)}, u32[]{:S(2)}, u32[]{:S(2)}) collective-permute-start(f32[2,4,128]{2,1,0:T(4,128)S(1)} %get-tuple-element.127), channel_id=1, source_target_pairs={{0,2},{2,4},{4,6},{1,3},{3,5},{5,7},{8,10},{10,12},{12,14},{9,11},... | collective-permute-start | bytes 12296 | tf_op jit(solution)/shard_map/ppermute | solution.py:25
  65.7 4.1 %collective-permute-done.6 = f32[2,4,128]{2,1,0:T(4,128)S(1)} collective-permute-done((f32[2,4,128]{2,1,0:T(4,128)S(1)}, f32[2,4,128]{2,1,0:T(4,128)S(1)}, u32[]{:S(2)}, u32[]{:S(2)}) %collective-permute-start.6) | collective-permute-done | bytes 4128 | tf_op jit(solution)/shard_map/ppermute | solution.py:28
  79.9 4.3 %collective-permute-start.13 = (f32[2,4,128]{2,1,0:T(4,128)S(1)}, f32[2,4,128]{2,1,0:T(4,128)S(1)}, u32[]{:S(2)}, u32[]{:S(2)}) collective-permute-start(f32[2,4,128]{2,1,0:T(4,128)S(1)} %get-tuple-element.125), channel_id=1, source_target_pairs={{0,2},{2,4},{4,6},{1,3},{3,5},{5,7},{8,10},{10,12},{12,14},{9,11},... | collective-permute-start | bytes 12296 | tf_op jit(solution)/shard_map/ppermute | solution.py:25
  85.6 4.2 %collective-permute-done.14 = f32[2,4,128]{2,1,0:T(4,128)S(1)} collective-permute-done((f32[2,4,128]{2,1,0:T(4,128)S(1)}, f32[2,4,128]{2,1,0:T(4,128)S(1)}, u32[]{:S(2)}, u32[]{:S(2)}) %collective-permute-start.14) | collective-permute-done | bytes 4128 | tf_op jit(solution)/shard_map/ppermute | solution.py:28
  92.7 1.9 collective-permute-done.16
  99.0 11.8 %all_to_all.38 = f32[2,1,256,128]{3,0,1,2:T(2,128)S(1)} all-to-all(f32[2,1,256,128]{3,0,1,2:T(2,128)S(1)} %copy.28), channel_id=1, replica_groups=mesh['tm'=4,'sx'=4,'sy'=2] {'tm'}, dimensions={2} | all-to-all | bytes 524288 | tf_op jit(solution)/shard_map/all_to_all | solution.py:172
  112.0 8.5 %all_to_all.39 = f32[4,64,128]{2,1,0:T(8,128)S(1)} all-to-all(f32[4,64,128]{2,1,0:T(8,128)S(1)} %copy.33), channel_id=1, replica_groups=mesh['tm'=4,'sx'=4,'sy'=2] {'tm'}, dimensions={0} | all-to-all | bytes 262144 | tf_op jit(solution)/shard_map/all_to_all | solution.py:81
  121.5 3.2 %collective-permute-start.17 = (f32[256,128]{1,0:T(8,128)S(1)}, f32[256,128]{1,0:T(8,128)S(1)}, u32[]{:S(2)}, u32[]{:S(2)}) collective-permute-start(f32[256,128]{1,0:T(8,128)S(1)} %get-tuple-element.33), channel_id=1, source_target_pairs={{0,8},{8,16},{16,24},{1,9},{9,17},{17,25},{2,10},{10,18},{18,26},{... | collective-permute-start | bytes 393224 | tf_op jit(solution)/shard_map/ppermute | solution.py:17
  124.7 2.8 %collective-permute-start.18 = (f32[2,1,128]{2,1,0:T(1,128)S(1)}, f32[2,1,128]{2,1,0:T(1,128)S(1)}, u32[]{:S(2)}, u32[]{:S(2)}) collective-permute-start(f32[2,1,128]{2,1,0:T(1,128)S(1)} %get-tuple-element.121), channel_id=1, source_target_pairs={{0,2},{2,4},{4,6},{1,3},{3,5},{5,7},{8,10},{10,12},{12,14},{9,11},... | collective-permute-start | bytes 3080 | tf_op jit(solution)/shard_map/ppermute | solution.py:25
  128.8 14.9 %all-gather.1 = f32[1024,128]{1,0:T(8,128)S(1)} all-gather(f32[256,128]{1,0:T(8,128)S(1)} %fusion.121), channel_id=3, replica_groups=mesh['tm'=4,'sx'=4,'sy'=2] {'tm'}, dimensions={0}, use_global_device_ids=true | all-gather | bytes 655360 | tf_op jit(solution)/shard_map/all_gather | solution.py:146
  146.5 2.1 collective-permute-done.21
  150.0 3.3 %all-to-all-start.4 = ((f32[1,256,128]{2,0,1:T(1,128)}), f32[1,256,128]{2,0,1:T(1,128)S(1)}, u32[]{:S(2)}, u32[]{:S(2)}) async-start(f32[1,256,128]{2,0,1:T(1,128)} %bitcast.38), calls=%async_computation.4 | async-start | bytes 262144 | tf_op jit(solution)/shard_map/all_to_all | solution.py:157
  153.3 4.6 %collective-permute-start.26 = (f32[2,5,128]{2,1,0:T(8,128)S(1)}, f32[2,5,128]{2,1,0:T(8,128)S(1)}, u32[]{:S(2)}, u32[]{:S(2)}) collective-permute-start(f32[2,5,128]{2,1,0:T(8,128)S(1)} %get-tuple-element.133), channel_id=1, source_target_pairs={{0,2},{2,4},{4,6},{1,3},{3,5},{5,7},{8,10},{10,12},{12,14},{9,11},... | collective-permute-start | bytes 15368 | tf_op jit(solution)/shard_map/ppermute | solution.py:25
  161.3 4.5 %all-to-all-start.5 = ((f32[2,4,64,128]{3,2,0,1:T(8,128)}), f32[2,4,64,128]{3,2,0,1:T(8,128)S(1)}, u32[]{:S(2)}, u32[]{:S(2)}) async-start(f32[2,4,64,128]{3,2,0,1:T(8,128)} %copy.37), calls=%async_computation.5 | async-start | bytes 524288 | tf_op jit(solution)/shard_map/all_to_all | solution.py:69
  168.7 2.1 collective-permute-done.29
  171.1 3.4 %all-to-all-done.5 = f32[2,4,64,128]{3,2,0,1:T(8,128)S(1)} async-done(((f32[2,4,64,128]{3,2,0,1:T(8,128)}), f32[2,4,64,128]{3,2,0,1:T(8,128)S(1)}, u32[]{:S(2)}, u32[]{:S(2)}) %all-to-all-start.5) | async-done | bytes 262176 | tf_op jit(solution)/shard_map/all_to_all | solution.py:69
  174.5 4.3 %collective-permute-start.22 = (f32[2,4,128]{2,1,0:T(4,128)S(1)}, f32[2,4,128]{2,1,0:T(4,128)S(1)}, u32[]{:S(2)}, u32[]{:S(2)}) collective-permute-start(f32[2,4,128]{2,1,0:T(4,128)S(1)} %get-tuple-element.117), channel_id=1, source_target_pairs={{0,2},{2,4},{4,6},{1,3},{3,5},{5,7},{8,10},{10,12},{12,14},{9,11},... | collective-permute-start | bytes 12296 | tf_op jit(solution)/shard_map/ppermute | solution.py:25
  180.1 4.1 %collective-permute-done.23 = f32[2,4,128]{2,1,0:T(4,128)S(1)} collective-permute-done((f32[2,4,128]{2,1,0:T(4,128)S(1)}, f32[2,4,128]{2,1,0:T(4,128)S(1)}, u32[]{:S(2)}, u32[]{:S(2)}) %collective-permute-start.23) | collective-permute-done | bytes 4128 | tf_op jit(solution)/shard_map/ppermute | solution.py:28
  194.4 4.6 %collective-permute-start.30 = (f32[2,4,128]{2,1,0:T(4,128)S(1)}, f32[2,4,128]{2,1,0:T(4,128)S(1)}, u32[]{:S(2)}, u32[]{:S(2)}) collective-permute-start(f32[2,4,128]{2,1,0:T(4,128)S(1)} %get-tuple-element.115), channel_id=1, source_target_pairs={{0,2},{2,4},{4,6},{1,3},{3,5},{5,7},{8,10},{10,12},{12,14},{9,11},... | collective-permute-start | bytes 12296 | tf_op jit(solution)/shard_map/ppermute | solution.py:25
  200.3 4.2 %collective-permute-done.31 = f32[2,4,128]{2,1,0:T(4,128)S(1)} collective-permute-done((f32[2,4,128]{2,1,0:T(4,128)S(1)}, f32[2,4,128]{2,1,0:T(4,128)S(1)}, u32[]{:S(2)}, u32[]{:S(2)}) %collective-permute-start.31) | collective-permute-done | bytes 4128 | tf_op jit(solution)/shard_map/ppermute | solution.py:28
  207.3 2.1 collective-permute-done.33
  213.8 11.8 %all_to_all.80 = f32[2,1,256,128]{3,0,1,2:T(2,128)S(1)} all-to-all(f32[2,1,256,128]{3,0,1,2:T(2,128)S(1)} %copy.40), channel_id=1, replica_groups=mesh['tm'=4,'sx'=4,'sy'=2] {'tm'}, dimensions={2} | all-to-all | bytes 524288 | tf_op jit(solution)/shard_map/all_to_all | solution.py:172
  226.7 8.4 %all_to_all.81 = f32[4,64,128]{2,1,0:T(8,128)S(1)} all-to-all(f32[4,64,128]{2,1,0:T(8,128)S(1)} %copy.45), channel_id=1, replica_groups=mesh['tm'=4,'sx'=4,'sy'=2] {'tm'}, dimensions={0} | all-to-all | bytes 262144 | tf_op jit(solution)/shard_map/all_to_all | solution.py:81
  (171 shorter events, 69.0 us)
Async XLA Ops:
  0.0 32.6 %collective-permute-start = (f32[256,128]{1,0:T(8,128)}, f32[256,128]{1,0:T(8,128)S(1)}, u32[]{:S(2)}, u32[]{:S(2)}) collective-permute-start(f32[256,128]{1,0:T(8,128)} %bitcast.172), channel_id=1, source_target_pairs={{0,8},{8,16},{16,24},{1,9},{9,17},{17,25},{2,10},{10,18},{18,26},{... | collective-permute-start | bytes 393224 | tf_op jit(solution)/shard_map/ppermute | solution.py:17
  6.1 21.1 %collective-permute-start.1 = (f32[2,1,128]{2,1,0:T(1,128)S(1)}, f32[2,1,128]{2,1,0:T(1,128)S(1)}, u32[]{:S(2)}, u32[]{:S(2)}) collective-permute-start(f32[2,1,128]{2,1,0:T(1,128)S(1)} %get-tuple-element.131), channel_id=1, source_target_pairs={{0,2},{2,4},{4,6},{1,3},{3,5},{5,7},{8,10},{10,12},{12,14},{9,11},... | collective-permute-start | bytes 3080 | tf_op jit(solution)/shard_map/ppermute | solution.py:25
  9.5 17.7 %collective-permute-start.2 = (f32[2,1,128]{2,1,0:T(1,128)S(1)}, f32[2,1,128]{2,1,0:T(1,128)S(1)}, u32[]{:S(2)}, u32[]{:S(2)}) collective-permute-start(f32[2,1,128]{2,1,0:T(1,128)S(1)} %get-tuple-element.132), channel_id=1, source_target_pairs={{2,0},{4,2},{6,4},{3,1},{5,3},{7,5},{10,8},{12,10},{14,12},{11,9},... | collective-permute-start | bytes 3080 | tf_op jit(solution)/shard_map/ppermute | solution.py:28
  28.8 3.4 %collective-permute-start.4 = (f32[2,258,1]{2,1,0:T(8,128)S(1)}, f32[2,258,1]{2,1,0:T(8,128)S(1)}, u32[]{:S(2)}, u32[]{:S(2)}) collective-permute-start(f32[2,258,1]{2,1,0:T(8,128)S(1)} %get-tuple-element.112), channel_id=1, source_target_pairs={{1,0},{3,2},{5,4},{7,6},{9,8},{11,10},{13,12},{15,14},{17,16},{19,... | collective-permute-start | bytes 6200 | tf_op jit(solution)/shard_map/ppermute | solution.py:28
  34.6 9.8 %all-to-all-start = ((f32[1,256,128]{2,0,1:T(1,128)}), f32[1,256,128]{2,0,1:T(1,128)S(1)}, u32[]{:S(2)}, u32[]{:S(2)}) async-start(f32[1,256,128]{2,0,1:T(1,128)} %bitcast.8), calls=%async_computation | async-start | bytes 262144 | tf_op jit(solution)/shard_map/all_to_all | solution.py:157
  37.9 13.2 %collective-permute-start.10 = (f32[2,5,128]{2,1,0:T(8,128)S(1)}, f32[2,5,128]{2,1,0:T(8,128)S(1)}, u32[]{:S(2)}, u32[]{:S(2)}) collective-permute-start(f32[2,5,128]{2,1,0:T(8,128)S(1)} %get-tuple-element.61), channel_id=1, source_target_pairs={{2,0},{4,2},{6,4},{3,1},{5,3},{7,5},{10,8},{12,10},{14,12},{11,9},... | collective-permute-start | bytes 15368 | tf_op jit(solution)/shard_map/ppermute | solution.py:28
  39.2 11.9 %collective-permute-start.9 = (f32[2,5,128]{2,1,0:T(8,128)S(1)}, f32[2,5,128]{2,1,0:T(8,128)S(1)}, u32[]{:S(2)}, u32[]{:S(2)}) collective-permute-start(f32[2,5,128]{2,1,0:T(8,128)S(1)} %get-tuple-element.136), channel_id=1, source_target_pairs={{0,2},{2,4},{4,6},{1,3},{3,5},{5,7},{8,10},{10,12},{12,14},{9,11},... | collective-permute-start | bytes 15368 | tf_op jit(solution)/shard_map/ppermute | solution.py:25
  46.1 13.7 %all-to-all-start.1 = ((f32[2,4,64,128]{3,2,0,1:T(8,128)}), f32[2,4,64,128]{3,2,0,1:T(8,128)S(1)}, u32[]{:S(2)}, u32[]{:S(2)}) async-start(f32[2,4,64,128]{3,2,0,1:T(8,128)} %copy.25), calls=%async_computation.1 | async-start | bytes 524288 | tf_op jit(solution)/shard_map/all_to_all | solution.py:69
  52.6 3.5 %collective-permute-start.12 = (f32[2,266,5]{2,1,0:T(8,128)S(1)}, f32[2,266,5]{2,1,0:T(8,128)S(1)}, u32[]{:S(2)}, u32[]{:S(2)}) collective-permute-start(f32[2,266,5]{2,1,0:T(8,128)S(1)} %get-tuple-element.92), channel_id=1, source_target_pairs={{1,0},{3,2},{5,4},{7,6},{9,8},{11,10},{13,12},{15,14},{17,16},{19,... | collective-permute-start | bytes 31928 | tf_op jit(solution)/shard_map/ppermute | solution.py:28
  59.8 5.9 %collective-permute-start.5 = (f32[2,4,128]{2,1,0:T(4,128)S(1)}, f32[2,4,128]{2,1,0:T(4,128)S(1)}, u32[]{:S(2)}, u32[]{:S(2)}) collective-permute-start(f32[2,4,128]{2,1,0:T(4,128)S(1)} %get-tuple-element.127), channel_id=1, source_target_pairs={{0,2},{2,4},{4,6},{1,3},{3,5},{5,7},{8,10},{10,12},{12,14},{9,11},... | collective-permute-start | bytes 12296 | tf_op jit(solution)/shard_map/ppermute | solution.py:25
  64.3 5.5 %collective-permute-start.6 = (f32[2,4,128]{2,1,0:T(4,128)S(1)}, f32[2,4,128]{2,1,0:T(4,128)S(1)}, u32[]{:S(2)}, u32[]{:S(2)}) collective-permute-start(f32[2,4,128]{2,1,0:T(4,128)S(1)} %get-tuple-element.128), channel_id=1, source_target_pairs={{2,0},{4,2},{6,4},{3,1},{5,3},{7,5},{10,8},{12,10},{14,12},{11,9},... | collective-permute-start | bytes 12296 | tf_op jit(solution)/shard_map/ppermute | solution.py:28
  70.0 3.1 %collective-permute-start.7 = (f32[2,264,4]{2,1,0:T(8,128)S(1)}, f32[2,264,4]{2,1,0:T(8,128)S(1)}, u32[]{:S(2)}, u32[]{:S(2)}) collective-permute-start(f32[2,264,4]{2,1,0:T(8,128)S(1)} %get-tuple-element.109), channel_id=1, source_target_pairs={{0,1},{2,3},{4,5},{6,7},{8,9},{10,11},{12,13},{14,15},{16,17},{18,... | collective-permute-start | bytes 25352 | tf_op jit(solution)/shard_map/ppermute | solution.py:25
  71.3 3.4 %collective-permute-start.8 = (f32[2,264,4]{2,1,0:T(8,128)S(1)}, f32[2,264,4]{2,1,0:T(8,128)S(1)}, u32[]{:S(2)}, u32[]{:S(2)}) collective-permute-start(f32[2,264,4]{2,1,0:T(8,128)S(1)} %get-tuple-element.110), channel_id=1, source_target_pairs={{1,0},{3,2},{5,4},{7,6},{9,8},{11,10},{13,12},{15,14},{17,16},{19,... | collective-permute-start | bytes 25352 | tf_op jit(solution)/shard_map/ppermute | solution.py:28
  79.9 5.6 %collective-permute-start.13 = (f32[2,4,128]{2,1,0:T(4,128)S(1)}, f32[2,4,128]{2,1,0:T(4,128)S(1)}, u32[]{:S(2)}, u32[]{:S(2)}) collective-permute-start(f32[2,4,128]{2,1,0:T(4,128)S(1)} %get-tuple-element.125), channel_id=1, source_target_pairs={{0,2},{2,4},{4,6},{1,3},{3,5},{5,7},{8,10},{10,12},{12,14},{9,11},... | collective-permute-start | bytes 12296 | tf_op jit(solution)/shard_map/ppermute | solution.py:25
  84.3 5.5 %collective-permute-start.14 = (f32[2,4,128]{2,1,0:T(4,128)S(1)}, f32[2,4,128]{2,1,0:T(4,128)S(1)}, u32[]{:S(2)}, u32[]{:S(2)}) collective-permute-start(f32[2,4,128]{2,1,0:T(4,128)S(1)} %get-tuple-element.126), channel_id=1, source_target_pairs={{2,0},{4,2},{6,4},{3,1},{5,3},{7,5},{10,8},{12,10},{14,12},{11,9},... | collective-permute-start | bytes 12296 | tf_op jit(solution)/shard_map/ppermute | solution.py:28
  91.2 3.4 %collective-permute-start.16 = (f32[2,264,4]{2,1,0:T(8,128)S(1)}, f32[2,264,4]{2,1,0:T(8,128)S(1)}, u32[]{:S(2)}, u32[]{:S(2)}) collective-permute-start(f32[2,264,4]{2,1,0:T(8,128)S(1)} %get-tuple-element.107), channel_id=1, source_target_pairs={{1,0},{3,2},{5,4},{7,6},{9,8},{11,10},{13,12},{15,14},{17,16},{19,... | collective-permute-start | bytes 25352 | tf_op jit(solution)/shard_map/ppermute | solution.py:28
  121.5 27.5 %collective-permute-start.17 = (f32[256,128]{1,0:T(8,128)S(1)}, f32[256,128]{1,0:T(8,128)S(1)}, u32[]{:S(2)}, u32[]{:S(2)}) collective-permute-start(f32[256,128]{1,0:T(8,128)S(1)} %get-tuple-element.33), channel_id=1, source_target_pairs={{0,8},{8,16},{16,24},{1,9},{9,17},{17,25},{2,10},{10,18},{18,26},{... | collective-permute-start | bytes 393224 | tf_op jit(solution)/shard_map/ppermute | solution.py:17
  124.7 19.0 %collective-permute-start.18 = (f32[2,1,128]{2,1,0:T(1,128)S(1)}, f32[2,1,128]{2,1,0:T(1,128)S(1)}, u32[]{:S(2)}, u32[]{:S(2)}) collective-permute-start(f32[2,1,128]{2,1,0:T(1,128)S(1)} %get-tuple-element.121), channel_id=1, source_target_pairs={{0,2},{2,4},{4,6},{1,3},{3,5},{5,7},{8,10},{10,12},{12,14},{9,11},... | collective-permute-start | bytes 3080 | tf_op jit(solution)/shard_map/ppermute | solution.py:25
  127.5 16.2 %collective-permute-start.19 = (f32[2,1,128]{2,1,0:T(1,128)S(1)}, f32[2,1,128]{2,1,0:T(1,128)S(1)}, u32[]{:S(2)}, u32[]{:S(2)}) collective-permute-start(f32[2,1,128]{2,1,0:T(1,128)S(1)} %get-tuple-element.122), channel_id=1, source_target_pairs={{2,0},{4,2},{6,4},{3,1},{5,3},{7,5},{10,8},{12,10},{14,12},{11,9},... | collective-permute-start | bytes 3080 | tf_op jit(solution)/shard_map/ppermute | solution.py:28
  145.2 3.4 %collective-permute-start.21 = (f32[2,258,1]{2,1,0:T(8,128)S(1)}, f32[2,258,1]{2,1,0:T(8,128)S(1)}, u32[]{:S(2)}, u32[]{:S(2)}) collective-permute-start(f32[2,258,1]{2,1,0:T(8,128)S(1)} %get-tuple-element.102), channel_id=1, source_target_pairs={{1,0},{3,2},{5,4},{7,6},{9,8},{11,10},{13,12},{15,14},{17,16},{19,... | collective-permute-start | bytes 6200 | tf_op jit(solution)/shard_map/ppermute | solution.py:28
  150.0 9.7 %all-to-all-start.4 = ((f32[1,256,128]{2,0,1:T(1,128)}), f32[1,256,128]{2,0,1:T(1,128)S(1)}, u32[]{:S(2)}, u32[]{:S(2)}) async-start(f32[1,256,128]{2,0,1:T(1,128)} %bitcast.38), calls=%async_computation.4 | async-start | bytes 262144 | tf_op jit(solution)/shard_map/all_to_all | solution.py:157
  153.3 12.6 %collective-permute-start.26 = (f32[2,5,128]{2,1,0:T(8,128)S(1)}, f32[2,5,128]{2,1,0:T(8,128)S(1)}, u32[]{:S(2)}, u32[]{:S(2)}) collective-permute-start(f32[2,5,128]{2,1,0:T(8,128)S(1)} %get-tuple-element.133), channel_id=1, source_target_pairs={{0,2},{2,4},{4,6},{1,3},{3,5},{5,7},{8,10},{10,12},{12,14},{9,11},... | collective-permute-start | bytes 15368 | tf_op jit(solution)/shard_map/ppermute | solution.py:25
  157.9 8.0 %collective-permute-start.27 = (f32[2,5,128]{2,1,0:T(8,128)S(1)}, f32[2,5,128]{2,1,0:T(8,128)S(1)}, u32[]{:S(2)}, u32[]{:S(2)}) collective-permute-start(f32[2,5,128]{2,1,0:T(8,128)S(1)} %get-tuple-element.134), channel_id=1, source_target_pairs={{2,0},{4,2},{6,4},{3,1},{5,3},{7,5},{10,8},{12,10},{14,12},{11,9},... | collective-permute-start | bytes 15368 | tf_op jit(solution)/shard_map/ppermute | solution.py:28
  161.3 13.1 %all-to-all-start.5 = ((f32[2,4,64,128]{3,2,0,1:T(8,128)}), f32[2,4,64,128]{3,2,0,1:T(8,128)S(1)}, u32[]{:S(2)}, u32[]{:S(2)}) async-start(f32[2,4,64,128]{3,2,0,1:T(8,128)} %copy.37), calls=%async_computation.5 | async-start | bytes 524288 | tf_op jit(solution)/shard_map/all_to_all | solution.py:69
  167.4 3.5 %collective-permute-start.29 = (f32[2,266,5]{2,1,0:T(8,128)S(1)}, f32[2,266,5]{2,1,0:T(8,128)S(1)}, u32[]{:S(2)}, u32[]{:S(2)}) collective-permute-start(f32[2,266,5]{2,1,0:T(8,128)S(1)} %get-tuple-element.90), channel_id=1, source_target_pairs={{1,0},{3,2},{5,4},{7,6},{9,8},{11,10},{13,12},{15,14},{17,16},{19,... | collective-permute-start | bytes 31928 | tf_op jit(solution)/shard_map/ppermute | solution.py:28
  174.5 5.6 %collective-permute-start.22 = (f32[2,4,128]{2,1,0:T(4,128)S(1)}, f32[2,4,128]{2,1,0:T(4,128)S(1)}, u32[]{:S(2)}, u32[]{:S(2)}) collective-permute-start(f32[2,4,128]{2,1,0:T(4,128)S(1)} %get-tuple-element.117), channel_id=1, source_target_pairs={{0,2},{2,4},{4,6},{1,3},{3,5},{5,7},{8,10},{10,12},{12,14},{9,11},... | collective-permute-start | bytes 12296 | tf_op jit(solution)/shard_map/ppermute | solution.py:25
  178.8 5.5 %collective-permute-start.23 = (f32[2,4,128]{2,1,0:T(4,128)S(1)}, f32[2,4,128]{2,1,0:T(4,128)S(1)}, u32[]{:S(2)}, u32[]{:S(2)}) collective-permute-start(f32[2,4,128]{2,1,0:T(4,128)S(1)} %get-tuple-element.118), channel_id=1, source_target_pairs={{2,0},{4,2},{6,4},{3,1},{5,3},{7,5},{10,8},{12,10},{14,12},{11,9},... | collective-permute-start | bytes 12296 | tf_op jit(solution)/shard_map/ppermute | solution.py:28
  184.4 3.3 %collective-permute-start.24 = (f32[2,264,4]{2,1,0:T(8,128)S(1)}, f32[2,264,4]{2,1,0:T(8,128)S(1)}, u32[]{:S(2)}, u32[]{:S(2)}) collective-permute-start(f32[2,264,4]{2,1,0:T(8,128)S(1)} %get-tuple-element.99), channel_id=1, source_target_pairs={{0,1},{2,3},{4,5},{6,7},{8,9},{10,11},{12,13},{14,15},{16,17},{18,... | collective-permute-start | bytes 25352 | tf_op jit(solution)/shard_map/ppermute | solution.py:25
  185.8 3.4 %collective-permute-start.25 = (f32[2,264,4]{2,1,0:T(8,128)S(1)}, f32[2,264,4]{2,1,0:T(8,128)S(1)}, u32[]{:S(2)}, u32[]{:S(2)}) collective-permute-start(f32[2,264,4]{2,1,0:T(8,128)S(1)} %get-tuple-element.100), channel_id=1, source_target_pairs={{1,0},{3,2},{5,4},{7,6},{9,8},{11,10},{13,12},{15,14},{17,16},{19,... | collective-permute-start | bytes 25352 | tf_op jit(solution)/shard_map/ppermute | solution.py:28
  194.4 5.9 %collective-permute-start.30 = (f32[2,4,128]{2,1,0:T(4,128)S(1)}, f32[2,4,128]{2,1,0:T(4,128)S(1)}, u32[]{:S(2)}, u32[]{:S(2)}) collective-permute-start(f32[2,4,128]{2,1,0:T(4,128)S(1)} %get-tuple-element.115), channel_id=1, source_target_pairs={{0,2},{2,4},{4,6},{1,3},{3,5},{5,7},{8,10},{10,12},{12,14},{9,11},... | collective-permute-start | bytes 12296 | tf_op jit(solution)/shard_map/ppermute | solution.py:25
  199.0 5.5 %collective-permute-start.31 = (f32[2,4,128]{2,1,0:T(4,128)S(1)}, f32[2,4,128]{2,1,0:T(4,128)S(1)}, u32[]{:S(2)}, u32[]{:S(2)}) collective-permute-start(f32[2,4,128]{2,1,0:T(4,128)S(1)} %get-tuple-element.116), channel_id=1, source_target_pairs={{2,0},{4,2},{6,4},{3,1},{5,3},{7,5},{10,8},{12,10},{14,12},{11,9},... | collective-permute-start | bytes 12296 | tf_op jit(solution)/shard_map/ppermute | solution.py:28
  206.0 3.4 %collective-permute-start.33 = (f32[2,264,4]{2,1,0:T(8,128)S(1)}, f32[2,264,4]{2,1,0:T(8,128)S(1)}, u32[]{:S(2)}, u32[]{:S(2)}) collective-permute-start(f32[2,264,4]{2,1,0:T(8,128)S(1)} %get-tuple-element.97), channel_id=1, source_target_pairs={{1,0},{3,2},{5,4},{7,6},{9,8},{11,10},{13,12},{15,14},{17,16},{19,... | collective-permute-start | bytes 25352 | tf_op jit(solution)/shard_map/ppermute | solution.py:28
  (12 other events, 22.0 us)
